TPU v7x, 32 devices: a whole 2x2x4 slice. The times are simulated.
32 devices in a mesh: band: 8 (over y, x, core), ga: 4 (over z).
Axes of the slice: x: 2, y: 2, z: 4, core: 2. Of those that a mesh axis runs over, the one named last changes fastest.
Arguments:
- orbitals: bfloat16 [256, 90112], P(('band', 'ga')), may hold values from -6 to 6
- local_part: bfloat16 [256, 90112], P(('band', 'ga')), may hold values from -6 to 6
- projectors: bfloat16 [90112, 1664], P(('band', 'ga')), may hold values from -0.01953125 to 0.01953125
- couplings: float32 [4, 13, 13], replicated, may hold values from -20 to 20, as said below
- species: int32 [128], replicated, may hold values from 0 to 3
Outputs:
- applied: bfloat16 [256, 90112], P(('band', 'ga'))
Inputs may be any that keep to these rules, and one draw needn't show every extreme that they name: `couplings`: each species has one symmetric block.
All inputs are finite; a program needn't handle non-finite values.
Results may differ from a plain program's by a relative error of at most 0.0056.
Values may be sent and summed in bfloat16 or wider, within the bound.
A program may use at most 64 MiB of HBM per device.

v0:
```python
import jax
import jax.numpy as jnp
from jax import lax
from jax.sharding import PartitionSpec as P


def select_blocks(couplings, species):
    kinds = couplings.shape[0]
    width = couplings.shape[1]
    select = (jnp.arange(kinds, dtype=jnp.int32)[:, None] == species[None, :]).astype(jnp.float32)
    table = jnp.einsum(
        "sk,sa->ka",
        couplings.reshape(kinds, width * width),
        select,
        precision=lax.Precision.HIGHEST,
    )
    return table.reshape(width, width, species.shape[0])


def couple(totals, blocks):
    width = blocks.shape[0]
    atom_count = blocks.shape[2]
    folded = totals.reshape(totals.shape[0], width, atom_count)
    mixed = jnp.zeros_like(folded)
    for inner in range(width):
        mixed = mixed + folded[:, inner, None, :] * blocks[None, inner, :, :]
    return mixed.reshape(totals.shape[0], width * atom_count).astype(jnp.bfloat16)


def expand(coefs, projectors):
    return jnp.einsum("bp,gp->bg", coefs, projectors, preferred_element_type=jnp.float32).astype(
        jnp.bfloat16
    )


def on_device(orbitals, local_part, projectors, couplings, species):
    blocks = select_blocks(couplings, species)
    slab_orbitals = lax.all_to_all(
        orbitals, ("band", "ga"), split_axis=1, concat_axis=0, tiled=True
    )
    partial_value = jnp.dot(slab_orbitals, projectors, preferred_element_type=jnp.float32)
    devices = lax.axis_size(("band", "ga"))
    pieces = lax.all_to_all(
        partial_value.astype(jnp.bfloat16), ("band", "ga"), split_axis=0, concat_axis=0, tiled=True
    )
    pieces = pieces.reshape(devices, pieces.shape[0] // devices, pieces.shape[1])
    totals = jnp.sum(pieces.astype(jnp.float32), axis=0)
    coefs = lax.all_gather(couple(totals, blocks), ("band", "ga"), axis=0, tiled=True)
    slab_correction = expand(coefs, projectors)
    correction = lax.all_to_all(
        slab_correction, ("band", "ga"), split_axis=0, concat_axis=1, tiled=True
    )
    correction = lax.optimization_barrier(correction)
    return (local_part.astype(jnp.float32) + correction.astype(jnp.float32)).astype(jnp.bfloat16)


def solution(mesh):
    placed = (P(("band", "ga"), None), P(("band", "ga"), None), P(("band", "ga"), None), P(), P())
    return jax.shard_map(
        on_device, mesh=mesh, in_specs=placed, out_specs=P(("band", "ga"), None), check_vma=False
    )
```

profile of v0, /device:TPU:1, one launch (start us, length us, event | category | flops | bytes accessed | tf_op | source)
XLA Modules:
  0.0 192.5 jit_solution(15892471655889466248)
XLA Ops:
  0.0 42.4 %all_to_all.47 = bf16[8,32,2816]{2,0,1:T(8,128)(2,1)S(1)} all-to-all(bf16[8,32,2816]{2,0,1:T(8,128)(2,1)} %bitcast.149), channel_id=1, replica_groups=mesh['band'=8,'ga'=4] {'band','ga'}, dimensions={1} | all-to-all | bytes 2883584 | tf_op jit(solution)/shard_map/all_to_all | solution.py:38
  42.4 7.3 %fusion.1 = bf16[32,8,1664]{2,1,0:T(8,128)(2,1)} fusion(bf16[2816,1664]{1,0:T(8,128)(2,1)} %param.7, bf16[8,32,2816]{2,0,1:T(8,128)(2,1)S(1)} %all_to_all.47), kind=kOutput, calls=%fused_computation.4 | convolution fusion | flops 2399567872 | bytes 11665408 | tf_op jit(solution)/shard_map/dot_general | solution.py:41
  49.7 0.0 copy-start.1
  49.7 0.0 copy-start.2
  49.7 2.8 %all-to-all-start.1 = ((bf16[32,8,1664]{2,1,0:T(8,128)(2,1)}), bf16[32,8,1664]{2,1,0:T(8,128)(2,1)S(1)}, u32[]{:S(2)}, u32[]{:S(2)}) async-start(bf16[32,8,1664]{2,1,0:T(8,128)(2,1)} %fusion.1), calls=%async_computation.1 | async-start | bytes 1703936 | tf_op jit(solution)/shard_map/all_to_all | solution.py:43
  52.6 0.0 copy-done.1
  52.6 0.1 reshape.85
  52.7 0.0 copy-done.2
  52.7 0.3 convolution_bitcast_fusion
  53.0 21.8 %all-to-all-done.1 = bf16[32,8,1664]{2,1,0:T(8,128)(2,1)S(1)} async-done(((bf16[32,8,1664]{2,1,0:T(8,128)(2,1)}), bf16[32,8,1664]{2,1,0:T(8,128)(2,1)S(1)}, u32[]{:S(2)}, u32[]{:S(2)}) %all-to-all-start.1) | async-done | bytes 852000 | tf_op jit(solution)/shard_map/all_to_all | solution.py:43
  74.8 0.1 convert_reduce_fusion
  74.9 0.1 fusion.4
  75.0 67.2 %all_gather.3 = bf16[256,1664]{1,0:T(8,128)(2,1)S(1)} all-gather(bf16[8,1664]{1,0:T(8,128)(2,1)S(1)} %fusion.4), channel_id=1, replica_groups=mesh['band'=8,'ga'=4] {'band','ga'}, dimensions={0}, use_global_device_ids=true | all-gather | bytes 878592 | tf_op jit(solution)/shard_map/all_gather | solution.py:48
  142.2 6.5 %fusion = bf16[32,8,2816]{2,1,0:T(8,128)(2,1)S(1)} fusion(bf16[256,1664]{1,0:T(8,128)(2,1)S(1)} %all_gather.3, bf16[2816,1664]{1,0:T(8,128)(2,1)} %param.7), kind=kOutput, calls=%fused_computation.1 | convolution fusion | flops 2399862784 | bytes 11665408 | tf_op jit(solution)/shard_map/bp,gp->bg/dot_general | solution.py:31
  148.7 0.0 copy-start
  148.7 42.4 %all_to_all.48 = bf16[32,8,2816]{2,1,0:T(8,128)(2,1)S(1)} all-to-all(bf16[32,8,2816]{2,1,0:T(8,128)(2,1)S(1)} %fusion), channel_id=1, replica_groups=mesh['band'=8,'ga'=4] {'band','ga'}, dimensions={0} | all-to-all | bytes 2883584 | tf_op jit(solution)/shard_map/all_to_all | solution.py:50
  191.1 0.0 copy-done
  191.1 1.4 add_convert_fusion
  (3 shorter events, 0.0 us)
Async XLA Ops:
  49.7 2.9 %copy-start.1 = (f32[4,13,13]{2,0,1:T(4,128)S(1)}, f32[4,13,13]{2,0,1:T(4,128)}, u32[]{:S(2)}) copy-start(f32[4,13,13]{2,0,1:T(4,128)} %param.8) | copy-start | bytes 8116
  49.7 3.0 %copy-start.2 = (s32[128]{0:T(128)S(1)}, s32[128]{0:T(128)}, u32[]{:S(2)}) copy-start(s32[128]{0:T(128)} %param.9) | copy-start | bytes 1540
  49.7 25.0 %all-to-all-start.1 = ((bf16[32,8,1664]{2,1,0:T(8,128)(2,1)}), bf16[32,8,1664]{2,1,0:T(8,128)(2,1)S(1)}, u32[]{:S(2)}, u32[]{:S(2)}) async-start(bf16[32,8,1664]{2,1,0:T(8,128)(2,1)} %fusion.1), calls=%async_computation.1 | async-start | bytes 1703936 | tf_op jit(solution)/shard_map/all_to_all | solution.py:43
  148.7 42.4 %copy-start = (bf16[8,90112]{1,0:T(8,128)(2,1)S(1)}, bf16[8,90112]{1,0:T(8,128)(2,1)}, u32[]{:S(2)}) copy-start(bf16[8,90112]{1,0:T(8,128)(2,1)} %param.6) | copy-start | bytes 4325380
where the time goes:
time: 193 us
  blocking collectives  152 us (79%)
  waiting for transfers between devices  21.8 us (11%)
  matrix products  14.1 us (7%)
  starting transfers between devices  2.84 us (1%)
    all_gather x1, blocking collectives, on_device(): lax.all_gather(couple(totals, blocks), ('band', 'ga'), axis=0, tiled=True)  67.2 us
    all_to_all x1, blocking collectives, on_device(): lax.all_to_all(slab_correction, ('band', 'ga'), split_axis=0, concat_axis...  42.4 us
    all_to_all x1, blocking collectives, on_device(): lax.all_to_all(orbitals, ('band', 'ga'), split_axis=1, concat_axis=0, til...  42.4 us
    all_to_all x1, waiting for transfers between devices, on_device(): lax.all_to_all(partial_value.astype(jnp.bfloat16), ('band', 'ga'), split_...  21.8 us
    dot_general x1, matrix products, on_device(): jnp.dot(slab_orbitals, projectors, preferred_element_type=jnp.float32)  7.35 us
    dot_general x1, matrix products, expand(): jnp.einsum('bp,gp->bg', coefs, projectors, preferred_element_type=jnp.flo...  6.5 us
  transfers between devices with their start and end apart: 1, of which 1 were waited for; matrix products, arithmetic and copies ran while one was open for 0% of the time, Pallas kernels for 0%

commit v1 on v0

--- a/solution.py
+++ b/solution.py
@@ -47,8 +47,14 @@
     totals = jnp.sum(pieces.astype(jnp.float32), axis=0)
     coefs = lax.all_gather(couple(totals, blocks), ("band", "ga"), axis=0, tiled=True)
     slab_correction = expand(coefs, projectors)
-    correction = lax.all_to_all(
-        slab_correction, ("band", "ga"), split_axis=0, concat_axis=1, tiled=True
+    correction = jnp.concatenate(
+        lax.all_to_all(
+            jnp.stack(jnp.split(slab_correction, lax.axis_size(("band", "ga")), axis=0)),
+            ("band", "ga"),
+            0,
+            0,
+        ),
+        axis=1,
     )
     correction = lax.optimization_barrier(correction)
     return (local_part.astype(jnp.float32) + correction.astype(jnp.float32)).astype(jnp.bfloat16)

time: 193 us -> 193 us (level)
  no operation moved by 1% of the time
where the time goes in v1:
time: 193 us
  blocking collectives  152 us (79%)
  waiting for transfers between devices  21.8 us (11%)
  matrix products  14.1 us (7%)
  starting transfers between devices  2.84 us (1%)
    all_gather x1, blocking collectives, on_device(): lax.all_gather(couple(totals, blocks), ('band', 'ga'), axis=0, tiled=True)  67.2 us
    all_to_all x1, blocking collectives, on_device(): lax.all_to_all(jnp.stack(jnp.split(slab_correction, lax.axis_size(('band'...  42.4 us
    all_to_all x1, blocking collectives, on_device(): lax.all_to_all(orbitals, ('band', 'ga'), split_axis=1, concat_axis=0, til...  42.4 us
    all_to_all x1, waiting for transfers between devices, on_device(): lax.all_to_all(partial_value.astype(jnp.bfloat16), ('band', 'ga'), split_...  21.8 us
    dot_general x1, matrix products, on_device(): jnp.dot(slab_orbitals, projectors, preferred_element_type=jnp.float32)  7.35 us
    dot_general x1, matrix products, expand(): jnp.einsum('bp,gp->bg', coefs, projectors, preferred_element_type=jnp.flo...  6.46 us
  transfers between devices with their start and end apart: 1, of which 1 were waited for; matrix products, arithmetic and copies ran while one was open for 0% of the time, Pallas kernels for 0%

profile of v1, /device:TPU:1, one launch (start us, length us, event | category | flops | bytes accessed | tf_op | source)
XLA Modules:
  0.0 192.9 jit_solution(10892091289672235637)
XLA Ops:
  0.0 42.4 %all_to_all.33 = bf16[8,32,2816]{2,0,1:T(8,128)(2,1)S(1)} all-to-all(bf16[8,32,2816]{2,0,1:T(8,128)(2,1)} %bitcast.275), channel_id=1, replica_groups=mesh['band'=8,'ga'=4] {'band','ga'}, dimensions={1} | all-to-all | bytes 2883584 | tf_op jit(solution)/shard_map/all_to_all | solution.py:38
  42.4 7.3 %fusion = bf16[32,8,1664]{2,1,0:T(8,128)(2,1)} fusion(bf16[2816,1664]{1,0:T(8,128)(2,1)} %param.7, bf16[8,32,2816]{2,0,1:T(8,128)(2,1)S(1)} %all_to_all.33), kind=kOutput, calls=%fused_computation.3 | convolution fusion | flops 2399567872 | bytes 11665408 | tf_op jit(solution)/shard_map/dot_general | solution.py:41
  49.7 0.0 copy-start.1
  49.7 0.0 copy-start.2
  49.7 2.8 %all-to-all-start.1 = ((bf16[32,8,1664]{2,1,0:T(8,128)(2,1)}), bf16[32,8,1664]{2,1,0:T(8,128)(2,1)S(1)}, u32[]{:S(2)}, u32[]{:S(2)}) async-start(bf16[32,8,1664]{2,1,0:T(8,128)(2,1)} %fusion), calls=%async_computation.1 | async-start | bytes 1703936 | tf_op jit(solution)/shard_map/all_to_all | solution.py:43
  52.6 0.0 copy-done.1
  52.6 0.1 reshape.88
  52.7 0.0 copy-done.2
  52.7 0.3 convolution_bitcast_fusion
  53.0 21.8 %all-to-all-done.1 = bf16[32,8,1664]{2,1,0:T(8,128)(2,1)S(1)} async-done(((bf16[32,8,1664]{2,1,0:T(8,128)(2,1)}), bf16[32,8,1664]{2,1,0:T(8,128)(2,1)S(1)}, u32[]{:S(2)}, u32[]{:S(2)}) %all-to-all-start.1) | async-done | bytes 852000 | tf_op jit(solution)/shard_map/all_to_all | solution.py:43
  74.8 0.1 convert_reduce_fusion
  74.9 0.1 fusion.3
  75.0 67.2 %all_gather.3 = bf16[256,1664]{1,0:T(8,128)(2,1)S(1)} all-gather(bf16[8,1664]{1,0:T(8,128)(2,1)S(1)} %fusion.3), channel_id=1, replica_groups=mesh['band'=8,'ga'=4] {'band','ga'}, dimensions={0}, use_global_device_ids=true | all-gather | bytes 878592 | tf_op jit(solution)/shard_map/all_gather | solution.py:48
  142.2 6.5 %convolution_convert_fusion = bf16[256,2816]{1,0:T(8,128)(2,1)S(1)} fusion(bf16[256,1664]{1,0:T(8,128)(2,1)S(1)} %all_gather.3, bf16[2816,1664]{1,0:T(8,128)(2,1)} %param.7), kind=kOutput, calls=%fused_computation | convolution fusion | flops 2399862784 | bytes 11665408 | tf_op jit(solution)/shard_map/bp,gp->bg/dot_general | solution.py:31
  149.1 0.0 copy-start
  149.1 42.4 %all_to_all.34 = bf16[32,8,2816]{2,1,0:T(8,128)(2,1)S(1)} all-to-all(bf16[32,8,2816]{2,1,0:T(8,128)(2,1)S(1)} %constant_dynamic-update-slice_fusion), channel_id=1, replica_groups=mesh['band'=8,'ga'=4] {'band','ga'}, dimensions={0} | all-to-all | bytes 2883584 | tf_op jit(solution)/shard_map/all_to_all | solution.py:51
  191.5 0.0 copy-done
  191.5 1.4 add_convert_fusion
  (35 shorter events, 0.2 us)
Async XLA Ops:
  49.7 2.9 %copy-start.1 = (f32[4,13,13]{2,0,1:T(4,128)S(1)}, f32[4,13,13]{2,0,1:T(4,128)}, u32[]{:S(2)}) copy-start(f32[4,13,13]{2,0,1:T(4,128)} %param.8) | copy-start | bytes 8116
  49.7 3.0 %copy-start.2 = (s32[128]{0:T(128)S(1)}, s32[128]{0:T(128)}, u32[]{:S(2)}) copy-start(s32[128]{0:T(128)} %param.9) | copy-start | bytes 1540
  49.7 25.0 %all-to-all-start.1 = ((bf16[32,8,1664]{2,1,0:T(8,128)(2,1)}), bf16[32,8,1664]{2,1,0:T(8,128)(2,1)S(1)}, u32[]{:S(2)}, u32[]{:S(2)}) async-start(bf16[32,8,1664]{2,1,0:T(8,128)(2,1)} %fusion), calls=%async_computation.1 | async-start | bytes 1703936 | tf_op jit(solution)/shard_map/all_to_all | solution.py:43
  149.1 42.4 %copy-start = (bf16[8,90112]{1,0:T(8,128)(2,1)S(1)}, bf16[8,90112]{1,0:T(8,128)(2,1)}, u32[]{:S(2)}) copy-start(bf16[8,90112]{1,0:T(8,128)(2,1)} %param.6) | copy-start | bytes 4325380
